TPU v7x, 32 devices: a whole 2x2x4 slice. The times are simulated.
32 devices in a mesh: bank: 2 (over y), zero: 16 (over z, x, core).
Axes of the slice: x: 2, y: 2, z: 4, core: 2. Of those that a mesh axis runs over, the one named last changes fastest.
Arguments:
- train_down: float32 [16, 6400, 4096], P('bank', None, 'zero'), may hold values from -0.109375 to 0.109375
- other_down: bfloat16 [16, 6400, 4096], P('bank', None, 'zero'), may hold values from -0.0390625 to 0.0390625
- router_weight: float32 [4096, 16], P('zero', 'bank'), may hold values from -0.09375 to 0.09375
- router_gain: float32 [4096], P('zero'), may hold values from 0.25 to 1.75
Outputs:
- ready_down: bfloat16 [16, 6400, 4096], P('bank', 'zero')
- scale_down: float32 [16, 6400], P('bank', 'zero')
- serve_router: bfloat16 [4096, 16], replicated
All inputs are finite; a program needn't handle non-finite values. Where the computation divides by a largest or mean magnitude, that divisor is 1e-20 or more.
Results may differ from a plain program's by a relative error of at most 0.001.
Values may be sent and summed in bfloat16 or wider, within the bound.
A program may use at most 256 MiB of HBM per device.

v0:
```python
import jax
import jax.numpy as jnp
from jax import lax
from jax.sharding import PartitionSpec as P


def local(train_down, other_down, router_weight, router_gain):
    latest_down = train_down + other_down.astype(jnp.float32)
    scale_down = lax.pmax(jnp.max(jnp.abs(latest_down), axis=2), "zero")
    narrow_down = (latest_down / jnp.expand_dims(scale_down, 2)).astype(jnp.bfloat16)
    ready_down = lax.all_to_all(narrow_down, "zero", split_axis=1, concat_axis=2, tiled=True)
    scale_down = lax.dynamic_slice_in_dim(
        scale_down, lax.axis_index("zero") * ready_down.shape[1], ready_down.shape[1], axis=1
    )
    part_router = (router_weight * router_gain[:, None]).astype(jnp.bfloat16)
    row_router = lax.all_gather(part_router, "zero", axis=0, tiled=True)
    serve_router = lax.all_gather(row_router, "bank", axis=1, tiled=True)
    return (ready_down, scale_down, serve_router)


def solution(mesh):
    in_specs = (P("bank", None, "zero"), P("bank", None, "zero"), P("zero", "bank"), P("zero"))
    out_specs = (P("bank", "zero", None), P("bank", "zero"), P())
    return jax.shard_map(local, mesh=mesh, in_specs=in_specs, out_specs=out_specs, check_vma=False)
```

profile of v0, /device:TPU:8, one launch (start us, length us, event | category | flops | bytes accessed | tf_op | source)
XLA Modules:
  0.0 938.4 jit_solution(1150257428159466706)
XLA Ops:
  7.2 0.0 all-reduce.2.cloned.1.call-start
  7.2 86.6 %abs_reduce_fusion = f32[8,6400]{0,1:T(8,128)} fusion(f32[8,6400,256]{2,1,0:T(8,128)} %param.4, bf16[8,6400,256]{2,1,0:T(8,128)(2,1)} %param.5), kind=kLoop, calls=%fused_computation.2 | loop fusion | flops 52377600 | bytes 78848000 | tf_op jit(solution)/shard_map/reduce_max | solution.py:9
  93.8 0.0 all-reduce.2.cloned.1.call-update
  93.8 106.0 %all-reduce.2.cloned.1.call-done = f32[8,6400]{0,1:T(8,128)} async-done(((f32[8,6400]{0,1:T(8,128)}), f32[8,6400]{0,1:T(8,128)}) %all-reduce.2.cloned.1.call-update) | async-done | bytes 204816 | tf_op jit(solution)/shard_map/pmax | solution.py:9
  199.8 86.4 %divide_convert_fusion = bf16[8,6400,256]{2,0,1:T(8,128)(2,1)} fusion(f32[8,6400,256]{2,1,0:T(8,128)} %param.4, f32[8,6400]{0,1:T(8,128)} %all-reduce.2.cloned.1.call-done, bf16[8,6400,256]{2,1,0:T(8,128)(2,1)} %param.5), kind=kLoop, calls=%fused_computation.1 | loop fusion | flops 52428800 | bytes 105062400 | tf_op jit(solution)/shard_map/convert_element_type | solution.py:10
  286.2 0.0 copy-start
  286.2 0.0 copy-start.1
  286.2 6.1 all-to-all-start
  292.3 0.0 copy-done
  292.4 0.0 copy-done.1
  292.4 574.6 %all_gather.6 = bf16[4096,8]{0,1:T(8,128)(2,1)S(1)} all-gather(bf16[256,8]{0,1:T(8,128)(2,1)S(1)} %multiply_convert_fusion), channel_id=1, replica_groups=mesh['bank'=2,'zero'=16] {'zero'}, dimensions={0}, use_global_device_ids=true | all-gather | bytes 69632 | tf_op jit(solution)/shard_map/all_gather | solution.py:16
  867.0 5.0 all_gather.7
  872.0 0.9 constant_dynamic-slice_fusion
  872.9 0.7 copy.15
  873.7 0.0 all-to-all-done
  873.7 18.1 %copy.14 = bf16[8,400,16,256]{3,2,1,0:T(8,128)(2,1)} copy(bf16[8,400,16,256]{3,0,1,2:T(8,128)(2,1)} %bitcast.1) | data formatting | bytes 52428800 | tf_op jit(solution)/shard_map/all_to_all | solution.py:11
  891.7 39.2 %all_to_all.16 = bf16[8,400,4096]{2,1,0:T(8,128)(2,1)} reshape(bf16[8,400,16,256]{3,2,1,0:T(8,128)(2,1)} %copy.14) | data formatting | bytes 52428800 | tf_op jit(solution)/shard_map/all_to_all | solution.py:11
  930.9 0.7 copy.25
  (1 shorter events, 0.0 us)
Async XLA Ops:
  7.2 192.7 %all-reduce.2.cloned.1.call-start = ((), (), s32[]{:S(2)}) async-start(), calls=%async_computation.1 | async-start | bytes 6553600 | tf_op jit(solution)/shard_map/pmax | solution.py:9
  286.2 6.1 copy-start
  286.2 6.1 copy-start.1
  286.2 587.4 %all-to-all-start = ((bf16[8,6400,256]{2,0,1:T(8,128)(2,1)}), bf16[8,6400,256]{2,0,1:T(8,128)(2,1)}, u32[]{:S(2)}, u32[]{:S(2)}) async-start(bf16[8,6400,256]{2,0,1:T(8,128)(2,1)} %divide_convert_fusion), calls=%async_computation | async-start | bytes 52428800 | tf_op jit(solution)/shard_map/all_to_all | solution.py:11
Sparse Core Ops, SparseCore 0:
  94.0 105.8 all-reduce.1
where the time goes:
time: 940 us; the launch traced here: 938 us
  blocking collectives  580 us (62%)
  other arithmetic  173 us (18%)
  waiting for transfers between devices  106 us (11%)
  local copies, waits for them, and re-layouts  59.6 us (6%)
  between operations  14.1 us (2%)
    all_gather x1, blocking collectives, local(): row_router = lax.all_gather(part_router, 'zero', axis=0, tiled=True)  575 us
    pmax x1, waiting for transfers between devices, local(): scale_down = lax.pmax(jnp.max(jnp.abs(latest_down), axis=2), 'zero')  106 us
    reduce_max x1, other arithmetic, local(): scale_down = lax.pmax(jnp.max(jnp.abs(latest_down), axis=2), 'zero')  86.6 us
    convert_element_type x1, other arithmetic, local(): (latest_down / jnp.expand_dims(scale_down, 2)).astype(jnp.bfloat16)  86.4 us
    all_to_all x2, local copies, waits for them, and re-layouts, local(): lax.all_to_all(narrow_down, 'zero', split_axis=1, concat_axis=2, tiled=True)  57.2 us
  transfers between devices with their start and end apart: 2, of which 1 were waited for; matrix products, arithmetic and copies ran while one was open for 0% of the time, Pallas kernels for 0%

commit v1 on v0

v1 whole, which is shorter than its diff:
```python
import functools

import jax
import jax.numpy as jnp
from jax import lax
from jax.experimental import pallas as pl
from jax.experimental.pallas import tpu as pltpu
from jax.sharding import PartitionSpec as P

MESH = pl.DeviceIdType.MESH
LANES = 128


def partner_of(me, step, count):
    if count & (count - 1):
        return lax.rem(me + step, count)
    other, bit = me, 1
    while bit < count:
        if step & bit:
            other = other + bit * (1 - 2 * lax.rem(lax.div(me, bit), 2))
        bit *= 2
    return other


def origin_of(me, step, count):
    if count & (count - 1):
        return lax.rem(me + count - step, count)
    return partner_of(me, step, count)


def kernel(count, train, other, ready, scale, t_buf, o_buf, narrow, peak, peaks, scales,
           load_sem, peak_send, peak_recv, scale_send, scale_recv, data_send, data_recv, own_sem):
    experts, _, rows, columns = train.shape
    starts = [min(LANES * i, rows - LANES) for i in range(pl.cdiv(rows, LANES))]
    blocks = len(starts)
    me, bank = lax.axis_index("zero"), lax.axis_index("bank")
    steps = list(range(count - 1, 0, -1))

    def loads(index):
        slot, expert = lax.rem(index, 2), lax.rem(index, experts)
        return (pltpu.make_async_copy(train.at[expert], t_buf.at[slot], load_sem.at[0, slot]),
                pltpu.make_async_copy(other.at[expert], o_buf.at[slot], load_sem.at[1, slot]))

    def remote(source, target, sends, receives, step):
        return pltpu.make_async_remote_copy(
            src_ref=source, dst_ref=target, send_sem=sends, recv_sem=receives,
            device_id=(bank, partner_of(me, step, count)), device_id_type=MESH)

    def latest(slot, part, start):
        span = pl.ds(start, LANES)
        return t_buf[slot, part, span, :] + o_buf[slot, part, span, :].astype(jnp.float32)

    def advance(index):
        @pl.when(index + 1 < 2 * experts)
        def _():
            for copy in loads(index + 1):
                copy.start()
        for copy in loads(index):
            copy.wait()

    for copy in loads(jnp.int32(0)):
        copy.start()
    barrier = pltpu.get_barrier_semaphore()
    for step in steps:
        pl.semaphore_signal(barrier, inc=1, device_id=(bank, partner_of(me, step, count)), device_id_type=MESH)

    @pl.loop(0, experts)
    def _(expert):
        advance(expert)
        slot = lax.rem(expert, 2)

        @pl.loop(0, count)
        def _(part):
            for block, start in enumerate(starts):
                value = jnp.abs(latest(slot, part, start))
                folded = value[:, :LANES]
                for column in range(LANES, columns, LANES):
                    folded = jnp.maximum(folded, value[:, column:column + LANES])
                peak[part, pl.ds(expert * blocks + block, 1), :] = jnp.max(folded.T, axis=0, keepdims=True)

    pl.semaphore_wait(barrier, count - 1)
    for step in steps:
        remote(peak.at[partner_of(me, step, count)], peaks.at[me], peak_send, peak_recv, step).start()
    pltpu.make_async_copy(peaks.at[pl.ds(0, count - 1)], peaks.at[pl.ds(0, count - 1)], peak_recv).wait()
    total = peak[me]
    for step in steps:
        total = jnp.maximum(total, peaks[origin_of(me, step, count)])
    scales[me] = total
    scale[...] = total
    for step in steps:
        remote(scales.at[me], scales.at[me], scale_send, scale_recv, step).start()
    pltpu.make_async_copy(scales.at[pl.ds(0, count - 1)], scales.at[pl.ds(0, count - 1)], scale_recv).wait()

    mine = pl.ds(pl.multiple_of(me * columns, LANES), columns)

    @pl.loop(0, experts)
    def _(expert):
        advance(expert + experts)
        slot = lax.rem(expert + experts, 2)

        @pl.loop(0, count)
        def _(part):
            for block, start in enumerate(starts):
                factor = 1.0 / scales[part, pl.ds(expert * blocks + block, 1), :]
                factor = jnp.broadcast_to(factor, (LANES, LANES)).T
                value = latest(slot, part, start)
                for column in range(0, columns, LANES):
                    narrow[expert, part, pl.ds(start, LANES), pl.ds(column, LANES)] = (
                        value[:, column:column + LANES] * factor).astype(narrow.dtype)

        for step in steps:
            remote(narrow.at[expert, partner_of(me, step, count)], ready.at[expert, :, mine],
                   data_send, data_recv, step).start()
        pltpu.make_async_copy(narrow.at[expert, me], ready.at[expert, :, mine], own_sem).start()

    pltpu.make_async_copy(peak.at[pl.ds(0, count - 1)], peak.at[pl.ds(0, count - 1)], peak_send).wait()
    pltpu.make_async_copy(peak.at[pl.ds(0, count - 1)], peak.at[pl.ds(0, count - 1)], scale_send).wait()
    sent = narrow.at[:, pl.ds(0, count - 1)]
    pltpu.make_async_copy(sent, sent, data_send).wait()
    pltpu.make_async_copy(narrow.at[:, 0], narrow.at[:, 0], own_sem).wait()
    got = ready.at[:, :, pl.ds(0, (count - 1) * columns)]
    pltpu.make_async_copy(got, got, data_recv).wait()


def local(count, train_down, other_down, router_weight, router_gain):
    experts, length, columns = train_down.shape
    rows = length // count
    blocks = pl.cdiv(rows, LANES)
    split = (experts, count, rows, columns)
    anywhere = pl.BlockSpec(memory_space=pl.ANY)
    ready_down, scale = pl.pallas_call(
        functools.partial(kernel, count),
        out_shape=(jax.ShapeDtypeStruct((experts, rows, count * columns), jnp.bfloat16),
                   jax.ShapeDtypeStruct((experts * blocks, LANES), jnp.float32)),
        in_specs=[anywhere, anywhere],
        out_specs=(anywhere, pl.BlockSpec(memory_space=pltpu.VMEM)),
        scratch_shapes=[
            pltpu.VMEM((2,) + split[1:], jnp.float32),
            pltpu.VMEM((2,) + split[1:], jnp.bfloat16),
            pltpu.VMEM(split, jnp.bfloat16),
            pltpu.VMEM((count, experts * blocks, LANES), jnp.float32),
            pltpu.VMEM((count, experts * blocks, LANES), jnp.float32),
            pltpu.VMEM((count, experts * blocks, LANES), jnp.float32),
            pltpu.SemaphoreType.DMA((2, 2)),
        ] + [pltpu.SemaphoreType.DMA] * 7,
        compiler_params=pltpu.CompilerParams(
            collective_id=0, has_side_effects=True, vmem_limit_bytes=60 * 1024 * 1024),
    )(train_down.reshape(split), other_down.reshape(split))
    scale = scale.reshape(experts, blocks, LANES)
    pieces = [scale[:, block] for block in range(blocks - 1)]
    scale_down = jnp.concatenate(pieces + [scale[:, blocks - 1, LANES * blocks - rows:]], axis=1)
    part_router = (router_weight * router_gain[:, None]).astype(jnp.bfloat16)
    row_router = lax.all_gather(part_router, "zero", axis=0, tiled=True)
    serve_router = lax.all_gather(row_router, "bank", axis=1, tiled=True)
    return (ready_down, scale_down, serve_router)


def solution(mesh):
    in_specs = (P("bank", None, "zero"), P("bank", None, "zero"), P("zero", "bank"), P("zero"))
    out_specs = (P("bank", "zero", None), P("bank", "zero"), P())
    body = functools.partial(local, mesh.shape["zero"])
    return jax.shard_map(body, mesh=mesh, in_specs=in_specs, out_specs=out_specs, check_vma=False)
```

time: 940 us -> 676 us (0.72)
  Pallas kernels: 0 us -> 626 us
  blocking collectives: 580 us -> 23.6 us
  other arithmetic: 173 us -> 0.62 us
  waiting for transfers between devices: 106 us -> 0 us
  local copies, waits for them, and re-layouts: 59.6 us -> 20.2 us
  between operations: 14.1 us -> 0.66 us
    pallas_call x0 -> x1, Pallas kernels: none -> 626 us  [local(): pl.pallas_call(functools.partial(kernel, count), out_shape=(jax.ShapeDtyp...]
    all_gather x1, blocking collectives: 575 us -> 18.6 us  [local(): row_router = lax.all_gather(part_router, 'zero', axis=0, tiled=True)]
    pmax x1 -> x0, waiting for transfers between devices: 106 us -> none  [local(): scale_down = lax.pmax(jnp.max(jnp.abs(latest_down), axis=2), 'zero')]
    reduce_max x1 -> x0, other arithmetic: 86.6 us -> none  [local(): scale_down = lax.pmax(jnp.max(jnp.abs(latest_down), axis=2), 'zero')]
    convert_element_type x1 -> x0, other arithmetic: 86.4 us -> none  [local(): (latest_down / jnp.expand_dims(scale_down, 2)).astype(jnp.bfloat16)]
    all_to_all x2 -> x0, local copies, waits for them, and re-layouts: 57.2 us -> none  [local(): lax.all_to_all(narrow_down, 'zero', split_axis=1, concat_axis=2, tiled=True)]
    unnamed x6, local copies, waits for them, and re-layouts: 1.37 us -> 18.6 us
  transfers between devices with their start and end apart: 2 -> 0, of which waited for: 1 -> 0; matrix products, arithmetic and copies ran while one was open for 0% -> 0% of each run, Pallas kernels for 0% -> 0%
where the time goes in v1:
time: 676 us; the launch traced here: 671 us
  Pallas kernels  626 us (93%)
  blocking collectives  23.6 us (3%)
  local copies, waits for them, and re-layouts  20.2 us (3%)
    pallas_call x1, Pallas kernels, local(): pl.pallas_call(functools.partial(kernel, count), out_shape=(jax.ShapeDtyp...  626 us
    all_gather x1, blocking collectives, local(): row_router = lax.all_gather(part_router, 'zero', axis=0, tiled=True)  18.6 us
    unnamed x6, local copies, waits for them, and re-layouts  18.6 us

profile of v1, /device:TPU:8, one launch (start us, length us, event | category | flops | bytes accessed | tf_op | source)
XLA Modules:
  0.0 670.9 jit_solution(14876392435584509725)
XLA Ops:
  0.6 0.0 copy-start
  0.6 0.0 copy-start.1
  0.7 625.8 %shard_map.67 = (bf16[8,400,4096]{2,1,0:T(8,128)(2,1)}, f32[32,128]{1,0:T(8,128)}) custom-call(f32[8,16,400,256]{3,2,1,0:T(8,128)} %bitcast.15, bf16[8,16,400,256]{3,2,1,0:T(8,128)(2,1)} %bitcast.16), custom_call_target="tpu_custom_call" | custom-call | tf_op jit(solution)/shard_map/pallas_call | solution.py:131
  626.4 0.8 fusion
  627.3 0.8 slice.19
  628.1 0.6 pad_maximum_fusion
  628.7 0.0 copy-done
  628.7 0.0 copy-done.1
  628.7 18.6 %all_gather.6 = bf16[4096,8]{0,1:T(8,128)(2,1)S(1)} all-gather(bf16[256,8]{0,1:T(8,128)(2,1)S(1)} %multiply_convert_fusion), channel_id=1, replica_groups=mesh['bank'=2,'zero'=16] {'zero'}, dimensions={0}, use_global_device_ids=true | all-gather | bytes 69632 | tf_op jit(solution)/shard_map/all_gather | solution.py:153
  647.3 5.0 all_gather.7
  652.3 17.9 %copy.17 = bf16[8,400,4096]{2,1,0:T(8,128)(2,1)} copy(bf16[8,400,4096]{2,1,0:T(8,128)(2,1)} %get-tuple-element.13) | data formatting | bytes 52428800
  670.3 0.7 copy.18
  (1 shorter events, 0.0 us)
Async XLA Ops:
  0.6 628.1 %copy-start = (f32[256,8]{0,1:T(8,128)S(1)}, f32[256,8]{0,1:T(8,128)}, u32[]{:S(2)}) copy-start(f32[256,8]{0,1:T(8,128)} %param.6) | copy-start | bytes 24580
  0.6 628.1 %copy-start.1 = (f32[256]{0:T(256)S(1)}, f32[256]{0:T(256)}, u32[]{:S(2)}) copy-start(f32[256]{0:T(256)} %param.7) | copy-start | bytes 3076

commit v2 on v1

v2 whole, which is shorter than its diff:
```python
import functools

import jax
import jax.numpy as jnp
from jax import lax
from jax.experimental import pallas as pl
from jax.experimental.pallas import tpu as pltpu
from jax.sharding import PartitionSpec as P

MESH = pl.DeviceIdType.MESH
LANES = 128


def partner_of(me, step, count):
    if count & (count - 1):
        return lax.rem(me + step, count)
    other, bit = me, 1
    while bit < count:
        if step & bit:
            other = other + bit * (1 - 2 * lax.rem(lax.div(me, bit), 2))
        bit *= 2
    return other


def origin_of(me, step, count):
    if count & (count - 1):
        return lax.rem(me + count - step, count)
    return partner_of(me, step, count)


def kernel(count, banks, train, other, weight, gain, ready, scale, router, t_buf, o_buf, narrow, pieces, gathered,
           peak_a, peaks_a, scales_a, peak_b, peaks_b, scales_b, load_sem, peak_send, peak_recv, scale_send, scale_recv,
           bank_send, bank_recv, router_send, router_recv, data_send, data_recv, own_sem):
    experts, _, rows, columns = train.shape
    starts = [min(LANES * i, rows - LANES) for i in range(pl.cdiv(rows, LANES))]
    blocks = len(starts)
    lead = lead_of(experts)
    me, bank = lax.axis_index("zero"), lax.axis_index("bank")
    steps = list(range(count - 1, 0, -1))
    groups = ((0, peak_a, peaks_a, scales_a), (lead, peak_b, peaks_b, scales_b))

    def loads(expert, slot):
        return (pltpu.make_async_copy(train.at[expert], t_buf.at[slot], load_sem.at[0, slot]),
                pltpu.make_async_copy(other.at[expert], o_buf.at[slot], load_sem.at[1, slot]))

    def remote(source, target, sends, receives, step):
        return pltpu.make_async_remote_copy(
            src_ref=source, dst_ref=target, send_sem=sends, recv_sem=receives,
            device_id=(bank, partner_of(me, step, count)), device_id_type=MESH)

    def settle(ref, semaphore):
        pltpu.make_async_copy(ref, ref, semaphore).wait()

    def latest(slot, part, start):
        span = pl.ds(start, LANES)
        return t_buf[slot, part, span, :] + o_buf[slot, part, span, :].astype(jnp.float32)

    def find_peaks(group, expert, slot):
        first, peak, _, _ = groups[group]

        @pl.loop(0, count)
        def _(part):
            for block, start in enumerate(starts):
                value = jnp.abs(latest(slot, part, start))
                folded = value[:, :LANES]
                for column in range(LANES, columns, LANES):
                    folded = jnp.maximum(folded, value[:, column:column + LANES])
                peak[part, pl.ds((expert - first) * blocks + block, 1), :] = jnp.max(folded.T, axis=0, keepdims=True)

    mine = pl.ds(pl.multiple_of(me * columns, LANES), columns)

    def normalise(group, expert, slot):
        first, _, _, scales = groups[group]

        @pl.loop(0, count)
        def _(part):
            for block, start in enumerate(starts):
                factor = 1.0 / scales[part, pl.ds((expert - first) * blocks + block, 1), :]
                factor = jnp.broadcast_to(factor, (LANES, LANES)).T
                value = latest(slot, part, start)
                for column in range(0, columns, LANES):
                    narrow[expert, part, pl.ds(start, LANES), pl.ds(column, LANES)] = (
                        value[:, column:column + LANES] * factor).astype(narrow.dtype)

        for step in steps:
            remote(narrow.at[expert, partner_of(me, step, count)], ready.at[expert, :, mine],
                   data_send, data_recv, step).start()
        pltpu.make_async_copy(narrow.at[expert, me], ready.at[expert, :, mine], own_sem).start()

    def send_peaks(group):
        _, peak, peaks, _ = groups[group]
        for step in steps:
            remote(peak.at[partner_of(me, step, count)], peaks.at[me],
                   peak_send.at[group], peak_recv.at[group], step).start()

    def send_scales(group):
        first, peak, peaks, scales = groups[group]
        settle(peaks.at[pl.ds(0, count - 1)], peak_recv.at[group])
        total = peak[me]
        for step in steps:
            total = jnp.maximum(total, peaks[origin_of(me, step, count)])
        scales[me] = total
        scale[pl.ds(first * blocks, total.shape[0]), :] = total
        for step in steps:
            remote(scales.at[me], scales.at[me], scale_send.at[group], scale_recv.at[group], step).start()

    def take_scales(group):
        scales = groups[group][3]
        settle(scales.at[pl.ds(0, count - 1)], scale_recv.at[group])

    def meet():
        pl.semaphore_wait(pltpu.get_barrier_semaphore(), count - 1 + banks - 1)
        for step in range(1, banks):
            pltpu.make_async_remote_copy(
                src_ref=pieces.at[bank], dst_ref=pieces.at[bank], send_sem=bank_send, recv_sem=bank_recv,
                device_id=(partner_of(bank, step, banks), me), device_id_type=MESH).start()
        send_peaks(0)

    def share_router():
        if banks > 1:
            settle(pieces.at[pl.ds(0, banks - 1)], bank_recv)
        gathered[me] = pieces[...]
        for step in steps:
            remote(pieces, gathered.at[me], router_send, router_recv, step).start()
        send_scales(0)

    near, far = min(lead + 1, experts), min(lead + 2, experts)
    rest = lead < experts
    plan = [
        (find_peaks, 0, 0, lead, meet),
        (find_peaks, 1, lead, near, share_router),
        (find_peaks, 1, near, far, lambda: take_scales(0)),
        (normalise, 0, 0, 1, None),
        (find_peaks, 1, far, experts, (lambda: send_peaks(1)) if rest else None),
        (normalise, 0, 1, min(2, lead), (lambda: send_scales(1)) if rest else None),
        (normalise, 0, min(2, lead), lead, (lambda: take_scales(1)) if rest else None),
        (normalise, 1, lead, experts, None),
    ]

    for copy in loads(0, 0):
        copy.start()
    barrier = pltpu.get_barrier_semaphore()
    for step in steps:
        pl.semaphore_signal(barrier, inc=1, device_id=(bank, partner_of(me, step, count)), device_id_type=MESH)
    for step in range(1, banks):
        pl.semaphore_signal(barrier, inc=1, device_id=(partner_of(bank, step, banks), me), device_id_type=MESH)
    pieces[bank] = (weight[...] * gain[...]).astype(pieces.dtype)

    place = 0
    for number, (work, group, first, last, then) in enumerate(plan):
        after = next((later[2] for later in plan[number + 1:] if later[2] < later[3]), None)

        def one(expert, position, coming):
            slot = lax.rem(position, 2)
            if coming is not None:
                for copy in loads(coming, 1 - slot):
                    copy.start()
            for copy in loads(expert, slot):
                copy.wait()
            work(group, expert, slot)

        if first < last:
            whole = last if after == last else last - 1
            if first < whole:
                @pl.loop(first, whole)
                def _(expert):
                    one(expert, expert - first + place, expert + 1)
            if whole < last:
                one(jnp.int32(whole), jnp.int32(whole - first + place), after)
            place += last - first
        if then is not None:
            then()

    for group in range(2 if rest else 1):
        peak = groups[group][1]
        settle(peak.at[pl.ds(0, count - 1)], peak_send.at[group])
        settle(peak.at[pl.ds(0, count - 1)], scale_send.at[group])
    if banks > 1:
        settle(pieces.at[pl.ds(0, banks - 1)], bank_send)
    settle(gathered.at[pl.ds(0, count - 1)], router_send)
    settle(gathered.at[pl.ds(0, count - 1)], router_recv)
    router[...] = gathered[...]
    settle(narrow.at[:, pl.ds(0, count - 1)], data_send)
    settle(narrow.at[:, 0], own_sem)
    settle(ready.at[:, :, pl.ds(0, (count - 1) * columns)], data_recv)


def lead_of(experts):
    return min(3, experts)


def local(count, banks, train_down, other_down, router_weight, router_gain):
    experts, length, columns = train_down.shape
    rows = length // count
    blocks = pl.cdiv(rows, LANES)
    split = (experts, count, rows, columns)
    share = (banks, router_weight.shape[1], router_weight.shape[0])
    lead = lead_of(experts)
    anywhere = pl.BlockSpec(memory_space=pl.ANY)
    inside = pl.BlockSpec(memory_space=pltpu.VMEM)
    tables = [pltpu.VMEM((count, blocks * size, LANES), jnp.float32)
              for size in (lead, max(experts - lead, 1)) for _ in range(3)]
    ready_down, scale, router = pl.pallas_call(
        functools.partial(kernel, count, banks),
        out_shape=(jax.ShapeDtypeStruct((experts, rows, count * columns), jnp.bfloat16),
                   jax.ShapeDtypeStruct((experts * blocks, LANES), jnp.float32),
                   jax.ShapeDtypeStruct((count,) + share, jnp.bfloat16)),
        in_specs=[anywhere, anywhere, inside, inside],
        out_specs=(anywhere, inside, inside),
        scratch_shapes=[
            pltpu.VMEM((2,) + split[1:], jnp.float32),
            pltpu.VMEM((2,) + split[1:], jnp.bfloat16),
            pltpu.VMEM(split, jnp.bfloat16),
            pltpu.VMEM(share, jnp.bfloat16),
            pltpu.VMEM((count,) + share, jnp.bfloat16),
        ] + tables + [pltpu.SemaphoreType.DMA((2, 2))] + [pltpu.SemaphoreType.DMA((2,))] * 4
        + [pltpu.SemaphoreType.DMA] * 7,
        compiler_params=pltpu.CompilerParams(
            collective_id=0, has_side_effects=True, vmem_limit_bytes=60 * 1024 * 1024),
    )(train_down.reshape(split), other_down.reshape(split), router_weight.T, router_gain[None, :])
    scale = scale.reshape(experts, blocks, LANES)
    parts = [scale[:, block] for block in range(blocks - 1)]
    scale_down = jnp.concatenate(parts + [scale[:, blocks - 1, LANES * blocks - rows:]], axis=1)
    serve_router = router.transpose(0, 3, 1, 2).reshape(count * share[2], banks * share[1])
    return (ready_down, scale_down, serve_router)


def solution(mesh):
    in_specs = (P("bank", None, "zero"), P("bank", None, "zero"), P("zero", "bank"), P("zero"))
    out_specs = (P("bank", "zero", None), P("bank", "zero"), P())
    body = functools.partial(local, mesh.shape["zero"], mesh.shape["bank"])
    return jax.shard_map(body, mesh=mesh, in_specs=in_specs, out_specs=out_specs, check_vma=False)
```

time: 676 us -> 633 us (0.936)
  blocking collectives: 23.6 us -> 0 us
  Pallas kernels: 626 us -> 607 us
    all_gather x2 -> x0, blocking collectives: 23.6 us -> none  [the longest x1 18.6 us: local(): row_router = lax.all_gather(part_router, 'zero', axis=0, tiled=True)]
    pallas_call x1, Pallas kernels: 626 us -> 607 us  [local(): pl.pallas_call(functools.partial(kernel, count, banks), out_shape=(jax.Sh...]
    unnamed x6 -> x2, local copies, waits for them, and re-layouts: 18.6 us -> 18.6 us
where the time goes in v2:
time: 633 us; the launch traced here: 629 us
  Pallas kernels  607 us (96%)
  local copies, waits for them, and re-layouts  21.2 us (3%)
    pallas_call x1, Pallas kernels, local(): pl.pallas_call(functools.partial(kernel, count, banks), out_shape=(jax.Sh...  607 us
    unnamed x2, local copies, waits for them, and re-layouts  18.6 us

profile of v2, /device:TPU:8, one launch (start us, length us, event | category | flops | bytes accessed | tf_op | source)
XLA Modules:
  0.0 629.4 jit_solution(3721302357491982379)
XLA Ops:
  0.6 607.0 %shard_map.67 = (bf16[8,400,4096]{2,1,0:T(8,128)(2,1)}, f32[32,128]{1,0:T(8,128)}, bf16[16,2,8,256]{3,2,1,0:T(8,128)(2,1)}) custom-call(f32[8,16,400,256]{3,2,1,0:T(8,128)} %bitcast.25, bf16[8,16,400,256]{3,2,1,0:T(8,128)(2,1)} %bitcast.26, f32[8,256]{1,0:T(8,128)} %bitcast.36, f32[1,256]{1,0:T(1,128)} %bitcast.37), custom_call_target="tpu_custom_call" | custom-call | tf_op jit(solution)/shard_map/pallas_call | solution.py:203
  607.6 0.8 slice.19
  608.4 0.8 fusion
  609.2 0.6 pad_maximum_fusion
  609.8 0.9 copy.22
  610.8 0.7 copy.20
  611.5 17.9 %copy.24 = bf16[8,400,4096]{2,1,0:T(8,128)(2,1)} copy(bf16[8,400,4096]{2,1,0:T(8,128)(2,1)} %get-tuple-element.15) | data formatting | bytes 52428800
